TPU v7x, 32 devices: a whole 2x2x4 slice. The times are simulated.
32 devices in a mesh: dp: 4 (over x, core), expert: 8 (over z, y).
Axes of the slice: x: 2, y: 2, z: 4, core: 2. Of those that a mesh axis runs over, the one named last changes fastest.
Arguments:
- tokens: bfloat16 [256, 7168], P('dp', 'expert'), parts along dimension 0, may hold values from -6 to 6
- routes: int32 [256, 8], P('dp'), parts along dimension 0, may hold values from 0 to 15, all different within a row; in each aligned block of 64 rows (0 to 63, 64 to 127, ...) at most 40 rows name the same one
- gate_values: bfloat16 [256, 8], P('dp'), parts along dimension 0, may hold values from 0.049804688 to 1
- gate_weight: bfloat16 [7168, 16384], P(None, 'expert'), may hold values from -0.0625 to 0.0625
- up_weight: bfloat16 [7168, 16384], P(None, 'expert'), may hold values from -0.0625 to 0.0625
- down_weight: bfloat16 [16384, 7168], P(None, 'expert'), may hold values from -0.1875 to 0.1875
Outputs:
- layer_output: bfloat16 [256, 7168], P('dp', 'expert'), parts along dimension 0
There are 4 independent parts, one for each index of `dp`. A program takes and returns all parts, laid end to end along the dimension named above; an argument that names none is the same for every part. Nothing has to cross between parts.
Inputs may be any that keep to these rules, and one draw needn't show every extreme that they name: `routes`: each row names 8 different experts; no expert is named by more than 40 rows of a group, a bound that some block reaches.
All inputs are finite; a program needn't handle non-finite values.
Results may differ from a plain program's by a relative error of at most 0.0049.
Values may be sent and summed in bfloat16 or wider, within the bound.
A program may use at most 128 MiB of HBM per device.

v0:
```python
import jax
import jax.numpy as jnp
from jax import lax
from jax.sharding import PartitionSpec as P

HIDDEN_SIZE = 1024
EXPERTS = 16


def body(tokens, routes, gate_values, gate_weight, up_weight, down_weight):
    unit_count = gate_weight.shape[1]
    span_units = min(unit_count, HIDDEN_SIZE)
    local_count = unit_count // span_units
    token_count = tokens.shape[0]
    first_expert = lax.axis_index("expert") * unit_count // HIDDEN_SIZE
    matched = routes[:, :, None] == lax.broadcasted_iota(jnp.int32, (1, 1, EXPERTS), 2)
    combine_table = jnp.sum(
        jnp.where(matched, gate_values[:, :, None].astype(jnp.float32), 0.0), axis=1
    )
    selector = (
        lax.broadcasted_iota(jnp.int32, (EXPERTS, local_count), 0)
        == first_expert + lax.broadcasted_iota(jnp.int32, (EXPERTS, local_count), 1)
    ).astype(jnp.float32)
    local_gates = jnp.dot(
        combine_table, selector, precision=lax.Precision.HIGHEST, preferred_element_type=jnp.float32
    )
    all_rows = lax.all_gather(tokens, "expert", axis=1, tiled=True)
    gate_proj = jnp.dot(all_rows, gate_weight, preferred_element_type=jnp.float32)
    up_proj = jnp.dot(all_rows, up_weight, preferred_element_type=jnp.float32)
    product = (jax.nn.silu(gate_proj) * up_proj).reshape(token_count, local_count, span_units)
    product = product * local_gates[:, :, None]
    hidden = product.reshape(token_count, unit_count).astype(jnp.bfloat16)
    result = jnp.dot(
        lax.all_gather(hidden, "expert", axis=1, tiled=True),
        down_weight,
        preferred_element_type=jnp.float32,
    )
    return result.astype(jnp.bfloat16)


def solution(mesh):
    in_specs = (
        P("dp", "expert"),
        P("dp", None),
        P("dp", None),
        P(None, "expert"),
        P(None, "expert"),
        P(None, "expert"),
    )
    out_specs = P("dp", "expert")
    return jax.shard_map(body, mesh=mesh, in_specs=in_specs, out_specs=out_specs, check_vma=False)
```

profile of v0, /device:TPU:0, one launch (start us, length us, event | category | flops | bytes accessed | tf_op | source)
XLA Modules:
  0.0 140.3 jit_solution(4098790935787080068)
XLA Ops:
  6.5 0.0 all-gather.2.cloned.1.call-start
  6.5 0.7 convert_element_type.11
  7.2 0.7 select_reduce_fusion
  7.9 0.2 fusion.2
  8.2 0.2 mul.24
  8.4 0.2 copy.12
  8.5 34.4 %all_gather.6 = bf16[64,7168]{1,0:T(8,128)(2,1)S(1)} all-gather(bf16[64,896]{1,0:T(8,128)(2,1)} %param.6), channel_id=1, replica_groups=mesh['dp'=4,'expert'=8] {'expert'}, dimensions={1}, use_global_device_ids=true | all-gather | bytes 1032192 | tf_op jit(solution)/shard_map/all_gather | solution.py:27
  42.9 12.1 %fusion.4 = f32[64,2048]{1,0:T(8,128)S(1)} fusion(bf16[64,7168]{1,0:T(8,128)(2,1)S(1)} %all_gather.6, bf16[7168,2048]{1,0:T(8,128)(2,1)} %param.9), kind=kOutput, calls=%fused_computation.10 | convolution fusion | flops 1879048192 | bytes 30801920 | tf_op jit(solution)/shard_map/dot_general | solution.py:28
  55.0 12.9 %fusion.1 = bf16[64,2048]{1,0:T(8,128)(2,1)} fusion(f32[64,2048]{1,0:T(8,128)S(1)} %bitcast.9, bf16[64,7168]{1,0:T(8,128)(2,1)S(1)} %all_gather.6, bf16[7168,2048]{1,0:T(8,128)(2,1)} %param.10, f32[64,2048]{1,0:T(8,128)S(1)} %fusion.4), kind=kOutput, calls=%fused_computation.2 | convolution fusion | flops 1879965696 | bytes 31588352 | tf_op jit(solution)/shard_map/dot_general | solution.py:29
  67.9 0.0 all-gather.2.cloned.1.call-update
  67.9 50.2 %all-gather.2.cloned.1.call-done = bf16[64,16384]{1,0:T(8,128)(2,1)} async-done(((bf16[64,2048]{1,0:T(8,128)(2,1)}), bf16[64,16384]{1,0:T(8,128)(2,1)}) %all-gather.2.cloned.1.call-update) | async-done | bytes 2097168 | tf_op jit(solution)/shard_map/all_gather | solution.py:34
  118.2 15.3 %convolution_convert_fusion = bf16[64,896]{1,0:T(8,128)(2,1)} fusion(bf16[64,16384]{1,0:T(8,128)(2,1)} %all-gather.2.cloned.1.call-done, bf16[16384,896]{1,0:T(8,128)(2,1)} %param.11), kind=kOutput, calls=%fused_computation.3 | convolution fusion | flops 1879105536 | bytes 31571968 | tf_op jit(solution)/shard_map/dot_general | solution.py:33
  (1 shorter events, 0.0 us)
Async XLA Ops:
  6.5 111.6 %all-gather.2.cloned.1.call-start = ((), (), s32[]{:S(2)}) async-start(), calls=%async_computation | async-start | bytes 2359296 | tf_op jit(solution)/shard_map/all_gather | solution.py:34
Sparse Core Ops, SparseCore 0:
  68.1 50.0 all-gather.1
where the time goes:
time: 140 us
  waiting for transfers between devices  50.3 us (36%)
  matrix products  40.5 us (29%)
  blocking collectives  34.4 us (25%)
  between operations  13.4 us (10%)
    all_gather x1, waiting for transfers between devices, body(): lax.all_gather(hidden, 'expert', axis=1, tiled=True)  50.2 us
    all_gather x1, blocking collectives, body(): all_rows = lax.all_gather(tokens, 'expert', axis=1, tiled=True)  34.4 us
    dot_general x1, matrix products, body(): jnp.dot(lax.all_gather(hidden, 'expert', axis=1, tiled=True), down_weight...  15.3 us
    dot_general x1, matrix products, body(): up_proj = jnp.dot(all_rows, up_weight, preferred_element_type=jnp.float32)  12.9 us
    dot_general x1, matrix products, body(): jnp.dot(all_rows, gate_weight, preferred_element_type=jnp.float32)  12.1 us
  transfers between devices with their start and end apart: 1, of which 1 were waited for; matrix products, arithmetic and copies ran while one was open for 0% of the time, Pallas kernels for 0%

commit v1 on v0

--- a/solution.py
+++ b/solution.py
@@ -1,13 +1,21 @@
+import functools
+
 import jax
 import jax.numpy as jnp
 from jax import lax
+from jax.experimental import pallas as pl
+from jax.experimental.pallas import tpu as pltpu
 from jax.sharding import PartitionSpec as P
 
 HIDDEN_SIZE = 1024
 EXPERTS = 16
-
-
-def body(tokens, routes, gate_values, gate_weight, up_weight, down_weight):
+CAP = 40
+TOKEN_PIECES = 2
+HIDDEN_PIECES = 2
+MESH = pl.DeviceIdType.MESH
+
+
+def plain_body(tokens, routes, gate_values, gate_weight, up_weight, down_weight):
     unit_count = gate_weight.shape[1]
     span_units = min(unit_count, HIDDEN_SIZE)
     local_count = unit_count // span_units
@@ -38,6 +46,286 @@
     return result.astype(jnp.bfloat16)
 
 
+def xor(a, b, bits):
+    total = 0
+    for i in range(bits):
+        p, q = (a // 2**i) % 2, (b // 2**i) % 2
+        total = total + (p + q - 2 * p * q) * 2**i
+    return total
+
+
+def kernel(
+    n,
+    tokens_hbm, routes_hbm, values_hbm, gate_hbm, up_hbm, down_hbm, out_ref,
+    x_buf, r_buf, v_buf, wg, wu, wd, h_buf, acc_g, acc_u, acc_o, other_o, slots,
+    local_sem, wg_sem, wu_sem, wd_sem,
+    xz_send, xy_send, xd_send, x_recv, xd_recv,
+    rv_send, rv_recv, hz_send, hy_send, h_recv, o_send, o_recv,
+):
+    d, e = lax.axis_index("dp"), lax.axis_index("expert")
+    core = d % 2
+    row, side = e // 2, e % 2
+    lines = n // 2
+    bits = lines.bit_length() - 1
+    rows, cols = x_buf.shape[2], x_buf.shape[3]
+    units = wg.shape[2]
+    both = 2 * rows
+    cap = h_buf.shape[2]
+    mate = {"dp": d + 1 - 2 * core}
+    f32, bf16 = jnp.float32, jnp.bfloat16
+
+    def source(k, crossed):
+        return 2 * xor(row, k, bits) + xor(side, crossed, 1)
+
+    def target(k, crossed):
+        return {"expert": source(k, crossed)}
+
+    def weight_copies(i):
+        who = source(i // 2, i % 2)
+        at = pl.ds(pl.multiple_of(who * cols, cols), cols)
+        mine = pl.ds(pl.multiple_of(core * units, units), units)
+        return (
+            pltpu.make_async_copy(gate_hbm.at[at, mine], wg.at[who], wg_sem.at[who]),
+            pltpu.make_async_copy(up_hbm.at[at, mine], wu.at[who], wu_sem.at[who]),
+        )
+
+    def down_copy(i):
+        who = source(i // 2, i % 2)
+        at = pl.ds(pl.multiple_of((2 * who + core) * units, units), units)
+        return pltpu.make_async_copy(down_hbm.at[at, :], wd.at[who], wd_sem.at[who])
+
+    own_copies = (
+        pltpu.make_async_copy(tokens_hbm, x_buf.at[core, e], local_sem.at[0]),
+        pltpu.make_async_copy(routes_hbm, r_buf.at[core], local_sem.at[1]),
+        pltpu.make_async_copy(values_hbm, v_buf.at[core], local_sem.at[2]),
+    )
+    for copy in own_copies:
+        copy.start()
+    for i in range(n):
+        for copy in weight_copies(i):
+            copy.start()
+    for i in range(n):
+        down_copy(i).start()
+
+    barrier = pltpu.get_barrier_semaphore()
+    for k in range(1, lines):
+        pl.semaphore_signal(barrier, inc=1, device_id=target(k, 0), device_id_type=MESH)
+    pl.semaphore_signal(barrier, inc=1, device_id=target(0, 1), device_id_type=MESH)
+    pl.semaphore_signal(barrier, inc=1, device_id=mate, device_id_type=MESH)
+    pl.semaphore_wait(barrier, lines + 1)
+
+    def remote(src, send, recv, device):
+        return pltpu.make_async_remote_copy(
+            src_ref=src, dst_ref=src, send_sem=send, recv_sem=recv,
+            device_id=device, device_id_type=MESH,
+        )
+
+    part = rows // TOKEN_PIECES
+
+    def x_piece(who, p):
+        return x_buf.at[core, who, pl.ds(p * part, part)]
+
+    def x_along(k, p):
+        return remote(x_piece(e, p), xz_send.at[k, p], x_recv.at[e, p], target(k, 0))
+
+    def x_across(k, p):
+        who = source(k, 0)
+        return remote(x_piece(who, p), xy_send.at[k, p], x_recv.at[who, p], target(0, 1))
+
+    def x_share(who, p):
+        return remote(x_piece(who, p), xd_send.at[who, p], xd_recv.at[who, p], mate)
+
+    def x_arrival(who, p):
+        return remote(x_piece(who, p), xd_send.at[who, p], x_recv.at[who, p], mate)
+
+    def x_shared(who, p):
+        there = x_buf.at[1 - core, who, pl.ds(p * part, part)]
+        return remote(there, xd_send.at[who, p], xd_recv.at[who, p], mate)
+
+    r_share = remote(r_buf.at[core], rv_send.at[0], rv_recv.at[0], mate)
+    v_share = remote(v_buf.at[core], rv_send.at[1], rv_recv.at[1], mate)
+
+    for copy in own_copies:
+        copy.wait()
+    for p in range(TOKEN_PIECES):
+        x_across(0, p).start()
+        for k in range(1, lines):
+            x_along(k, p).start()
+        x_share(e, p).start()
+    r_share.start()
+    v_share.start()
+    acc_g[...] = jnp.zeros_like(acc_g)
+    acc_u[...] = jnp.zeros_like(acc_u)
+    acc_o[...] = jnp.zeros_like(acc_o)
+    r_share.wait_recv()
+    v_share.wait_recv()
+
+    lane = lax.broadcasted_iota(jnp.int32, (both, 128), 1)
+    routed = r_buf[...].reshape(both, r_buf.shape[2])
+    values = v_buf[...].astype(f32).reshape(both, v_buf.shape[2])
+    named = jnp.zeros((both, 128), f32)
+    combine = jnp.zeros((both, 128), f32)
+    for k in range(routed.shape[1]):
+        hit = routed[:, k:k + 1] == lane
+        named = jnp.where(hit, 1.0, named)
+        combine = combine + jnp.where(hit, values[:, k:k + 1], 0.0)
+    t0 = lax.broadcasted_iota(jnp.int32, (both, both), 0)
+    t1 = lax.broadcasted_iota(jnp.int32, (both, both), 1)
+    earlier = jnp.where((t1 < t0) & ((t1 >= rows) == (t0 >= rows)), 1.0, 0.0)
+    rank = jnp.dot(earlier.astype(bf16), named.astype(bf16), preferred_element_type=f32)
+    base = jnp.where(lax.broadcasted_iota(jnp.int32, (both, 128), 0) >= rows, float(CAP), 0.0)
+    table = jnp.where(named > 0.0, rank + base, -1.0)
+    slots[...] = table
+    expert = 2 * e + core
+    sub = lax.broadcasted_iota(jnp.int32, (128, both), 0)
+    slot_row = jnp.sum(jnp.where(sub == expert, table.T, 0.0), axis=0, keepdims=True)
+    value_row = jnp.sum(jnp.where(sub == expert, combine.T, 0.0), axis=0, keepdims=True)
+    picked = slot_row == lax.broadcasted_iota(jnp.int32, (cap, both), 0).astype(f32)
+    pick = jnp.where(picked, 1.0, 0.0).astype(bf16)
+    weight = jnp.sum(jnp.where(picked, value_row, 0.0), axis=1, keepdims=True)
+
+    def gate_step(j, carry):
+        k, crossed = j // 2, j % 2
+        who = source(k, crossed)
+
+        @pl.when((crossed == 1) & (k + 1 < lines))
+        def _():
+            for p in range(TOKEN_PIECES):
+                coming = source(k + 1, 0)
+                x_arrival(coming, p).wait_recv()
+                x_across(k + 1, p).start()
+                x_share(coming, p).start()
+
+        @pl.when(crossed == 1)
+        def _():
+            for p in range(TOKEN_PIECES):
+                x_arrival(who, p).wait_recv()
+                x_share(who, p).start()
+
+        for p in range(TOKEN_PIECES):
+            x_shared(who, p).wait_recv()
+        for copy in weight_copies(j):
+            copy.wait()
+        x = jnp.concatenate([x_buf[0, who], x_buf[1, who]], axis=0)
+        xc = jnp.dot(pick, x, preferred_element_type=f32).astype(bf16)
+        acc_g[...] += jnp.dot(xc, wg[who], preferred_element_type=f32)
+        acc_u[...] += jnp.dot(xc, wu[who], preferred_element_type=f32)
+        return carry
+
+    lax.fori_loop(0, n, gate_step, 0)
+
+    def h_along(k, p):
+        return remote(h_buf.at[e, p], hz_send.at[k, p], h_recv.at[e, p], target(k, 0))
+
+    def h_across(k, p):
+        who = source(k, 0)
+        return remote(h_buf.at[who, p], hy_send.at[k, p], h_recv.at[who, p], target(0, 1))
+
+    def h_arrival(who, p):
+        return remote(h_buf.at[who, p], hy_send.at[0, p], h_recv.at[who, p], target(0, 1))
+
+    slab = units // HIDDEN_PIECES
+    for p in range(HIDDEN_PIECES):
+        at = slice(p * slab, (p + 1) * slab)
+        gate = acc_g[:, at]
+        hidden = gate / (1.0 + jnp.exp(-gate)) * acc_u[:, at] * weight
+        h_buf[e, p] = hidden.astype(bf16)
+        h_across(0, p).start()
+        for k in range(1, lines):
+            h_along(k, p).start()
+
+    def down_step(j, carry):
+        k, crossed = j // 2, j % 2
+        who = source(k, crossed)
+
+        @pl.when((crossed == 1) & (k + 1 < lines))
+        def _():
+            for p in range(HIDDEN_PIECES):
+                h_arrival(source(k + 1, 0), p).wait_recv()
+                h_across(k + 1, p).start()
+
+        @pl.when(crossed == 1)
+        def _():
+            for p in range(HIDDEN_PIECES):
+                h_arrival(who, p).wait_recv()
+
+        down_copy(j).wait()
+        lanes = lax.broadcasted_iota(jnp.int32, (both, 128), 1)
+        column = jnp.sum(
+            jnp.where(lanes == 2 * who + core, slots[...], 0.0), axis=1, keepdims=True
+        )
+        place = column == lax.broadcasted_iota(jnp.int32, (both, cap), 1).astype(f32)
+        place = jnp.where(place, 1.0, 0.0).astype(bf16)
+        for p in range(HIDDEN_PIECES):
+            full = jnp.dot(place, h_buf[who, p], preferred_element_type=f32).astype(bf16)
+            acc_o[...] += jnp.dot(
+                full, wd[who, pl.ds(p * slab, slab)], preferred_element_type=f32
+            ).reshape(acc_o.shape)
+        return carry
+
+    lax.fori_loop(0, n, down_step, 0)
+
+    back = pltpu.make_async_remote_copy(
+        src_ref=acc_o.at[1 - core], dst_ref=other_o, send_sem=o_send, recv_sem=o_recv,
+        device_id=mate, device_id_type=MESH,
+    )
+    back.start()
+    r_share.wait_send()
+    v_share.wait_send()
+    for p in range(TOKEN_PIECES):
+        for k in range(lines):
+            x_across(k, p).wait_send()
+        for k in range(1, lines):
+            x_along(k, p).wait_send()
+        for i in range(n):
+            x_share(i, p).wait_send()
+    for p in range(HIDDEN_PIECES):
+        for k in range(lines):
+            h_across(k, p).wait_send()
+        for k in range(1, lines):
+            h_along(k, p).wait_send()
+    back.wait()
+    out_ref[...] = (acc_o[core] + other_o[...]).astype(out_ref.dtype)
+
+
+def fused_body(n, tokens, routes, gate_values, gate_weight, up_weight, down_weight):
+    rows, cols = tokens.shape
+    units = gate_weight.shape[1] // 2
+    cap = 2 * CAP
+    lines = n // 2
+    dma = lambda *dims: pltpu.SemaphoreType.DMA(dims)
+    bf16, f32 = jnp.bfloat16, jnp.float32
+    return pl.pallas_call(
+        functools.partial(kernel, n),
+        out_shape=jax.ShapeDtypeStruct((rows, cols), bf16),
+        in_specs=[pl.BlockSpec(memory_space=pl.ANY)] * 6,
+        out_specs=pl.BlockSpec(memory_space=pltpu.VMEM),
+        scratch_shapes=[
+            pltpu.VMEM((2, n, rows, cols), bf16),
+            pltpu.VMEM((2,) + routes.shape, routes.dtype),
+            pltpu.VMEM((2,) + gate_values.shape, bf16),
+            pltpu.VMEM((n, cols, units), bf16),
+            pltpu.VMEM((n, cols, units), bf16),
+            pltpu.VMEM((n, units, cols), bf16),
+            pltpu.VMEM((n, HIDDEN_PIECES, cap, units // HIDDEN_PIECES), bf16),
+            pltpu.VMEM((cap, units), f32),
+            pltpu.VMEM((cap, units), f32),
+            pltpu.VMEM((2, rows, cols), f32),
+            pltpu.VMEM((rows, cols), f32),
+            pltpu.VMEM((2 * rows, 128), f32),
+            dma(3), dma(n), dma(n), dma(n),
+            dma(lines, TOKEN_PIECES), dma(lines, TOKEN_PIECES), dma(n, TOKEN_PIECES),
+            dma(n, TOKEN_PIECES), dma(n, TOKEN_PIECES),
+            dma(2), dma(2),
+            dma(lines, HIDDEN_PIECES), dma(lines, HIDDEN_PIECES), dma(n, HIDDEN_PIECES),
+            pltpu.SemaphoreType.DMA, pltpu.SemaphoreType.DMA,
+        ],
+        compiler_params=pltpu.CompilerParams(
+            collective_id=0, has_side_effects=True, vmem_limit_bytes=62 * 1024 * 1024
+        ),
+    )(tokens, routes, gate_values, gate_weight, up_weight, down_weight)
+
+
 def solution(mesh):
     in_specs = (
         P("dp", "expert"),
@@ -48,4 +336,16 @@
         P(None, "expert"),
     )
     out_specs = P("dp", "expert")
+    n = mesh.shape["expert"]
+    lines = n // 2
+
+    def body(*args):
+        tokens, gate_weight = args[0], args[3]
+        whole_experts = gate_weight.shape[1] == 2 * HIDDEN_SIZE
+        aligned = tokens.shape[1] % 128 == 0 and 2 * tokens.shape[0] == 128
+        paired = mesh.shape["dp"] % 2 == 0 and n % 2 == 0 and lines & (lines - 1) == 0
+        if whole_experts and aligned and paired and lines > 1:
+            return fused_body(n, *args)
+        return plain_body(*args)
+
     return jax.shard_map(body, mesh=mesh, in_specs=in_specs, out_specs=out_specs, check_vma=False)

time: 140 us -> 65.9 us (0.47)
  Pallas kernels: 0 us -> 61.4 us
  waiting for transfers between devices: 50.3 us -> 0 us
  matrix products: 40.5 us -> 0 us
  blocking collectives: 34.4 us -> 0 us
  between operations: 13.4 us -> 0.01 us
  local copies, waits for them, and re-layouts: 0.36 us -> 4.3 us
    pallas_call x0 -> x1, Pallas kernels: none -> 61.4 us  [fused_body(): pl.pallas_call(functools.partial(kernel, n), out_shape=jax.ShapeDtypeStru...]
    all_gather x1 -> x0, waiting for transfers between devices: 50.2 us -> none  [body(): lax.all_gather(hidden, 'expert', axis=1, tiled=True)]
    dot_general x4 -> x0, matrix products: 40.5 us -> none  [the longest x1 15.3 us: body(): jnp.dot(lax.all_gather(hidden, 'expert', axis=1, tiled=True), down_weight...]
    all_gather x1 -> x0, blocking collectives: 34.4 us -> none  [body(): all_rows = lax.all_gather(tokens, 'expert', axis=1, tiled=True)]
    unnamed x1 -> x3, local copies, waits for them, and re-layouts: 0.16 us -> 4.3 us
  transfers between devices with their start and end apart: 1 -> 0, of which waited for: 1 -> 0; matrix products, arithmetic and copies ran while one was open for 0% -> 0% of each run, Pallas kernels for 0% -> 0%
where the time goes in v1:
time: 65.9 us; the launch traced here: 65.7 us
  Pallas kernels  61.4 us (93%)
  local copies, waits for them, and re-layouts  4.3 us (7%)
    pallas_call x1, Pallas kernels, fused_body(): pl.pallas_call(functools.partial(kernel, n), out_shape=jax.ShapeDtypeStru...  61.4 us
    unnamed x3, local copies, waits for them, and re-layouts  4.3 us

profile of v1, /device:TPU:0, one launch (start us, length us, event | category | flops | bytes accessed | tf_op | source)
XLA Modules:
  0.0 65.7 jit_solution(17252746724376714287)
XLA Ops:
  0.0 1.4 %copy.8.values_hbm = bf16[64,8]{1,0:T(8,128)(2,1)} copy(bf16[64,8]{0,1:T(8,128)(2,1)} %param.8) | data formatting | bytes 2048 | tf_op args[2]
  1.4 1.4 %copy.7.routes_hbm = s32[64,8]{1,0:T(8,128)} copy(s32[64,8]{0,1:T(8,128)} %param.7) | data formatting | bytes 4096 | tf_op args[1]
  2.8 61.4 %shard_map.64 = bf16[64,896]{1,0:T(8,128)(2,1)} custom-call(bf16[64,896]{1,0:T(8,128)(2,1)} %tokens_hbm.1, s32[64,8]{1,0:T(8,128)} %copy.7.routes_hbm, bf16[64,8]{1,0:T(8,128)(2,1)} %copy.8.values_hbm, bf16[7168,2048]{1,0:T(8,128)(2,1)} %gate_hbm.1, bf16[7168,2048]{1,0:T(8,128)(2,1)} %up_hbm.1, bf16[16384,896]{1,0:T(8,128)(2,1)} %down_hbm.1), custom_call_target="tpu_custom_call" | custom-call | tf_op jit(solution)/shard_map/pallas_call | solution.py:298
  64.2 1.6 %copy.10 = bf16[64,896]{1,0:T(8,128)(2,1)} copy(bf16[64,896]{1,0:T(8,128)(2,1)} %shard_map.64) | data formatting | bytes 229376

commit v2 on v1

--- a/solution.py
+++ b/solution.py
@@ -10,8 +10,8 @@
 HIDDEN_SIZE = 1024
 EXPERTS = 16
 CAP = 40
-TOKEN_PIECES = 2
-HIDDEN_PIECES = 2
+TOKEN_PIECES = 1
+HIDDEN_PIECES = 1
 MESH = pl.DeviceIdType.MESH
 
 
@@ -101,11 +101,6 @@
     )
     for copy in own_copies:
         copy.start()
-    for i in range(n):
-        for copy in weight_copies(i):
-            copy.start()
-    for i in range(n):
-        down_copy(i).start()
 
     barrier = pltpu.get_barrier_semaphore()
     for k in range(1, lines):
@@ -154,32 +149,41 @@
         x_share(e, p).start()
     r_share.start()
     v_share.start()
+    for i in range(n):
+        for copy in weight_copies(i):
+            copy.start()
     acc_g[...] = jnp.zeros_like(acc_g)
     acc_u[...] = jnp.zeros_like(acc_u)
     acc_o[...] = jnp.zeros_like(acc_o)
     r_share.wait_recv()
     v_share.wait_recv()
 
-    lane = lax.broadcasted_iota(jnp.int32, (both, 128), 1)
-    routed = r_buf[...].reshape(both, r_buf.shape[2])
-    values = v_buf[...].astype(f32).reshape(both, v_buf.shape[2])
-    named = jnp.zeros((both, 128), f32)
-    combine = jnp.zeros((both, 128), f32)
-    for k in range(routed.shape[1]):
-        hit = routed[:, k:k + 1] == lane
-        named = jnp.where(hit, 1.0, named)
-        combine = combine + jnp.where(hit, values[:, k:k + 1], 0.0)
+    named = []
+    combine = []
+    for g in range(2):
+        expert_row = lax.broadcasted_iota(jnp.int32, (128, rows), 0)
+        hits = jnp.zeros((128, rows), f32)
+        shares = jnp.zeros((128, rows), f32)
+        values = v_buf[g].astype(f32)
+        for k in range(r_buf.shape[1]):
+            hit = r_buf[g, k:k + 1, :] == expert_row
+            hits = jnp.where(hit, 1.0, hits)
+            shares = jnp.where(hit, values[k:k + 1, :], shares)
+        named.append(hits)
+        combine.append(shares)
+    named = jnp.concatenate(named, axis=1)
+    combine = jnp.concatenate(combine, axis=1)
     t0 = lax.broadcasted_iota(jnp.int32, (both, both), 0)
     t1 = lax.broadcasted_iota(jnp.int32, (both, both), 1)
-    earlier = jnp.where((t1 < t0) & ((t1 >= rows) == (t0 >= rows)), 1.0, 0.0)
-    rank = jnp.dot(earlier.astype(bf16), named.astype(bf16), preferred_element_type=f32)
-    base = jnp.where(lax.broadcasted_iota(jnp.int32, (both, 128), 0) >= rows, float(CAP), 0.0)
+    earlier = jnp.where((t0 < t1) & ((t0 >= rows) == (t1 >= rows)), 1.0, 0.0)
+    rank = jnp.dot(named.astype(bf16), earlier.astype(bf16), preferred_element_type=f32)
+    base = jnp.where(lax.broadcasted_iota(jnp.int32, (128, both), 1) >= rows, float(CAP), 0.0)
     table = jnp.where(named > 0.0, rank + base, -1.0)
-    slots[...] = table
+    slots[...] = table.T
     expert = 2 * e + core
     sub = lax.broadcasted_iota(jnp.int32, (128, both), 0)
-    slot_row = jnp.sum(jnp.where(sub == expert, table.T, 0.0), axis=0, keepdims=True)
-    value_row = jnp.sum(jnp.where(sub == expert, combine.T, 0.0), axis=0, keepdims=True)
+    slot_row = jnp.sum(jnp.where(sub == expert, table, 0.0), axis=0, keepdims=True)
+    value_row = jnp.sum(jnp.where(sub == expert, combine, 0.0), axis=0, keepdims=True)
     picked = slot_row == lax.broadcasted_iota(jnp.int32, (cap, both), 0).astype(f32)
     pick = jnp.where(picked, 1.0, 0.0).astype(bf16)
     weight = jnp.sum(jnp.where(picked, value_row, 0.0), axis=1, keepdims=True)
@@ -206,6 +210,7 @@
             x_shared(who, p).wait_recv()
         for copy in weight_copies(j):
             copy.wait()
+        down_copy(j).start()
         x = jnp.concatenate([x_buf[0, who], x_buf[1, who]], axis=0)
         xc = jnp.dot(pick, x, preferred_element_type=f32).astype(bf16)
         acc_g[...] += jnp.dot(xc, wg[who], preferred_element_type=f32)
@@ -302,8 +307,8 @@
         out_specs=pl.BlockSpec(memory_space=pltpu.VMEM),
         scratch_shapes=[
             pltpu.VMEM((2, n, rows, cols), bf16),
-            pltpu.VMEM((2,) + routes.shape, routes.dtype),
-            pltpu.VMEM((2,) + gate_values.shape, bf16),
+            pltpu.VMEM((2,) + routes.shape[::-1], routes.dtype),
+            pltpu.VMEM((2,) + gate_values.shape[::-1], bf16),
             pltpu.VMEM((n, cols, units), bf16),
             pltpu.VMEM((n, cols, units), bf16),
             pltpu.VMEM((n, units, cols), bf16),
@@ -323,7 +328,7 @@
         compiler_params=pltpu.CompilerParams(
             collective_id=0, has_side_effects=True, vmem_limit_bytes=62 * 1024 * 1024
         ),
-    )(tokens, routes, gate_values, gate_weight, up_weight, down_weight)
+    )(tokens, routes.T, gate_values.T, gate_weight, up_weight, down_weight)
 
 
 def solution(mesh):

time: 65.9 us -> 48.9 us (0.74)
  Pallas kernels: 61.4 us -> 47.2 us
  local copies, waits for them, and re-layouts: 4.3 us -> 1.55 us
    pallas_call x1, Pallas kernels: 61.4 us -> 47.2 us  [fused_body(): pl.pallas_call(functools.partial(kernel, n), out_shape=jax.ShapeDtypeStru...]
    unnamed x3 -> x1, local copies, waits for them, and re-layouts: 4.3 us -> 1.55 us
where the time goes in v2:
time: 48.9 us; the launch traced here: 48.8 us
  Pallas kernels  47.2 us (97%)
  local copies, waits for them, and re-layouts  1.55 us (3%)
    pallas_call x1, Pallas kernels, fused_body(): pl.pallas_call(functools.partial(kernel, n), out_shape=jax.ShapeDtypeStru...  47.2 us
    unnamed x1, local copies, waits for them, and re-layouts  1.55 us

profile of v2, /device:TPU:0, one launch (start us, length us, event | category | flops | bytes accessed | tf_op | source)
XLA Modules:
  0.0 48.8 jit_solution(9482135619411371764)
XLA Ops:
  0.0 47.2 %shard_map.64 = bf16[64,896]{1,0:T(8,128)(2,1)} custom-call(bf16[64,896]{1,0:T(8,128)(2,1)} %tokens_hbm.1, s32[8,64]{1,0:T(8,128)} %bitcast.2, bf16[8,64]{1,0:T(8,128)(2,1)} %bitcast.3, bf16[7168,2048]{1,0:T(8,128)(2,1)} %gate_hbm.1, bf16[7168,2048]{1,0:T(8,128)(2,1)} %up_hbm.1, bf16[16384,896]{1,0:T(8,128)(2,1)} %down_hbm.1), custom_call_target="tpu_custom_call" | custom-call | tf_op jit(solution)/shard_map/pallas_call | solution.py:303
  47.2 1.6 %copy.8 = bf16[64,896]{1,0:T(8,128)(2,1)} copy(bf16[64,896]{1,0:T(8,128)(2,1)} %shard_map.64) | data formatting | bytes 229376
